TPU v7x, 256 devices: a whole 4x4x8 slice. The times are simulated.
256 devices in a mesh: section: 2 (over y_hi), dp: 16 (over z, core), vocab: 8 (over y_lo, x).
Axes of the slice: x: 4, y: 4 (y_hi: 2, y_lo: 2; y = y_hi * 2 + y_lo), z: 8, core: 2. Of those that a mesh axis runs over, the one named last changes fastest.
Arguments:
- activations: bfloat16 [2, 2048, 2048], P('section', 'dp'), may hold values from -32 to 32
- token_ids: int32 [2, 2048], replicated, may hold values from 0 to 65535
- embed_table: bfloat16 [65536, 2048], P(('dp', 'vocab')), may hold values from -3 to 3
Outputs:
- tied_grad: bfloat16 [128, 2, 256, 2048], P(('dp', 'vocab'), 'section')
All inputs are finite; a program needn't handle non-finite values.
Results may differ from a plain program's by a relative error of at most 0.0029.
Values may be sent and summed in bfloat16 or wider, within the bound.
No kernel may reach another device: no remote copies, remote signals or barrier semaphores. Data moves between devices by JAX's collectives and lax.ppermute only.
A program may use at most 128 MiB of HBM per device.

v0:
```python
import jax
import jax.numpy as jnp
from jax import lax
from jax.sharding import Mesh
from jax.sharding import PartitionSpec as P

DP = ("dp_0", "dp_1")
VOCAB = ("vocab_0", "vocab_1")
SECTION_DP_VOCAB = ("section", "dp_0", "dp_1", "vocab_0", "vocab_1")
DP_VOCAB = ("dp_0", "dp_1", "vocab_0", "vocab_1")


def from_partner(block, axis, apart):
    count = lax.axis_size(axis)
    route = []
    for low in range(count):
        high = low | 1 << apart
        if high != low and high < count:
            route += [(low, high), (high, low)]
    return lax.ppermute(block, axis, route)


def collected_together(shard, axis):
    leaves = jax.tree.leaves(shard)
    sequence = sorted(range(len(leaves)), key=lambda k: -leaves[k].size)
    width = (1, *leaves[sequence[0]].shape)[-1]
    lines = [
        jnp.pad(leaves[k].reshape(-1), (0, -leaves[k].size % width)).reshape(-1, width)
        for k in sequence
    ]
    both, at, found = (lax.all_gather(jnp.concatenate(lines), axis), 0, {})
    for k, line in zip(sequence, lines):
        share = both[:, at : at + len(line)].reshape(len(both), -1)
        found[k] = share[:, : leaves[k].size].reshape(-1, *leaves[k].shape)
        at += len(line)
    numbers = iter(range(len(leaves)))
    return jax.tree.map(lambda _: found[next(numbers)], shard)


def combined_by_axis(shard, axes, combine):
    for axis in axes:
        pieces = collected_together(shard, axis)
        shard = jax.tree.map(lambda part: part[0], pieces)
        for k in range(1, lax.axis_size(axis)):
            shard = combine(shard, jax.tree.map(lambda part: part[k], pieces))
    return shard


def combine(left_pair, right_pair):
    row_peak = jnp.maximum(left_pair[0], right_pair[0])
    row_total = left_pair[1] * jnp.exp(left_pair[0] - row_peak) + right_pair[1] * jnp.exp(
        right_pair[0] - row_peak
    )
    return (row_peak, row_total)


def spread_rows(row_tuple):
    return (
        lax.all_gather(row_tuple[0], DP, axis=0, tiled=True),
        lax.all_gather(row_tuple[1], DP, axis=0, tiled=True),
    )


def local_stats(logits):
    row_peak = jnp.max(logits, axis=1)
    row_total = jnp.sum(jnp.exp(logits - row_peak[:, None]), axis=1)
    return (row_peak, row_total)


def body(activations, token_ids, embed_table):
    own_rows = activations[0]
    model_width = own_rows.shape[1]
    table_count = embed_table.shape[0]
    section_index = lax.axis_index("section")
    half_rows = table_count // lax.axis_size("section")
    block_first = (lax.axis_index(DP) * lax.axis_size(VOCAB) + lax.axis_index(VOCAB)) * table_count
    partner = from_partner(own_rows, "section", 0)
    cot_rows = jnp.where(section_index == 0, own_rows, partner)
    hid_rows = jnp.where(section_index == 0, partner, own_rows)
    cot_all, hid_all = spread_rows((cot_rows, hid_rows))
    my_table = lax.dynamic_slice_in_dim(embed_table, section_index * half_rows, half_rows, 0)
    row_first = block_first + section_index * half_rows
    positions = jnp.arange(half_rows, dtype=jnp.int32)[None, :]
    target_hot = (token_ids[1] - row_first)[:, None] == positions
    input_hot = (token_ids[0] - row_first)[:, None] == positions
    logits = lax.dot_general(
        hid_all, my_table, (((1,), (1,)), ((), ())), preferred_element_type=jnp.float32
    )
    row_peak, row_total = local_stats(logits)
    peak_all, total_all = combined_by_axis((row_peak, row_total), SECTION_DP_VOCAB, combine)
    probs = jnp.exp(logits - peak_all[:, None]) / total_all[:, None]
    last_part = (probs - target_hot.astype(jnp.float32)).astype(jnp.bfloat16)
    first_part = input_hot.astype(jnp.bfloat16)
    summed = lax.dot_general(
        last_part, hid_all, (((0,), (0,)), ((), ())), preferred_element_type=jnp.float32
    )
    summed = summed + lax.dot_general(
        first_part, cot_all, (((0,), (0,)), ((), ())), preferred_element_type=jnp.float32
    )
    return summed.astype(jnp.bfloat16).reshape(1, 1, half_rows, model_width)


def solution(mesh):
    finer = Mesh(
        mesh.devices.reshape(mesh.shape["section"], 8, 2, 2, 4),
        ("section", "dp_0", "dp_1", "vocab_0", "vocab_1"),
    )
    in_specs = (P("section", DP, None), P(), P(DP_VOCAB, None))
    out_specs = P(DP_VOCAB, "section", None, None)
    return jax.shard_map(body, mesh=finer, in_specs=in_specs, out_specs=out_specs, check_vma=False)
```

profile of v0, /device:TPU:1, one launch (start us, length us, event | category | flops | bytes accessed | tf_op | source)
XLA Modules:
  0.0 161.4 jit_solution(14041888525596776392)
XLA Ops:
  6.5 0.0 copy-start
  6.5 0.0 all-gather.13.cloned.1.call-start
  6.5 3.7 %collective-permute-start = (bf16[128,2048]{1,0:T(8,128)(2,1)}, bf16[128,2048]{1,0:T(8,128)(2,1)S(1)}, u32[]{:S(2)}, u32[]{:S(2)}) collective-permute-start(bf16[128,2048]{1,0:T(8,128)(2,1)} %bitcast.264), channel_id=1, source_target_pairs={{0,128},{128,0},{1,129},{129,1},{2,130},{130,2},{3,131},{131,3},{4... | collective-permute-start | bytes 1572872 | tf_op jit(solution)/shard_map/ppermute | solution.py:20
  10.3 10.9 %collective-permute-done = bf16[128,2048]{1,0:T(8,128)(2,1)S(1)} collective-permute-done((bf16[128,2048]{1,0:T(8,128)(2,1)}, bf16[128,2048]{1,0:T(8,128)(2,1)S(1)}, u32[]{:S(2)}, u32[]{:S(2)}) %collective-permute-start) | collective-permute-done | bytes 524320 | tf_op jit(solution)/shard_map/ppermute | solution.py:20
  21.2 2.1 %broadcast_select_fusion.1 = (bf16[128,2048]{1,0:T(8,128)(2,1)}, bf16[128,2048]{1,0:T(8,128)(2,1)}) fusion(bf16[128,2048]{1,0:T(8,128)(2,1)S(1)} %collective-permute-done, pred[]{:T(512)S(6)} %eq.14, bf16[1,128,2048]{2,1,0:T(8,128)(2,1)} %param.3), kind=kLoop, calls=%fused_computation.15 | loop fusion | flops 524288 | bytes 2097153 | tf_op jit(solution)/shard_map/jit(_where)/select_n | solution.py:79
  23.3 0.0 all-gather.13.cloned.1.call-update
  23.3 0.0 all-gather.15.cloned.1.call-start
  23.4 0.7 all-gather.15.cloned.1.call-update
  24.1 60.1 %all-gather.13.cloned.1.call-done = bf16[2048,2048]{1,0:T(8,128)(2,1)} async-done(((bf16[128,2048]{1,0:T(8,128)(2,1)}), bf16[2048,2048]{1,0:T(8,128)(2,1)}) %all-gather.13.cloned.1.call-update) | async-done | bytes 8388624 | tf_op jit(solution)/shard_map/all_gather | solution.py:60
  84.2 0.0 copy-done
  84.2 5.8 %fusion.56 = (f32[2048]{0:T(1024)S(1)}, f32[2048,256]{0,1:T(8,128)S(1)}) fusion(bf16[2048,2048]{1,0:T(8,128)(2,1)} %all-gather.13.cloned.1.call-done, bf16[512,2048]{1,0:T(8,128)(2,1)S(1)} %copy-done, s32[]{:T(128)S(6)} %select_n.17), kind=kOutput, calls=%fused_computation.95 | convolution fusion | flops 2148005888 | bytes 11542532 | tf_op jit(solution)/shard_map/dot_general | solution.py:86
  90.0 0.0 copy-start.1
  90.0 1.3 copy-done.1
  91.3 0.3 exponential_reduce_fusion
  91.7 4.8 %all-gather.5 = f32[2,2,2048]{2,1,0:T(2,128)S(1)} all-gather(f32[1,2,2048]{2,1,0:T(2,128)S(1)} %maximum_bitcast_fusion), channel_id=2, replica_groups=mesh['section'=2,'dp_0'=8,'dp_1'=2,'vocab_0'=2,'vocab_1'=4] {'section'}, dimensions={0}, use_global_device_ids=true | all-gather | bytes 49152 | tf_op jit(solution)/shard_map/all_gather | solution.py:31
  96.5 21.3 %all-gather.6 = f32[8,2,2048]{2,1,0:T(2,128)S(1)} all-gather(f32[1,2,2048]{2,1,0:T(2,128)S(1)} %maximum_bitcast_fusion.1), channel_id=3, replica_groups=mesh['section'=2,'dp_0'=8,'dp_1'=2,'vocab_0'=2,'vocab_1'=4] {'dp_0'}, dimensions={0}, use_global_device_ids=true | all-gather | bytes 147456 | tf_op jit(solution)/shard_map/all_gather | solution.py:31
  117.8 0.2 fusion.16
  118.0 6.9 %all-gather.7 = f32[2,2,2048]{2,1,0:T(2,128)S(1)} all-gather(f32[1,2,2048]{2,1,0:T(2,128)S(1)} %maximum_bitcast_fusion.2), channel_id=4, replica_groups=mesh['section'=2,'dp_0'=8,'dp_1'=2,'vocab_0'=2,'vocab_1'=4] {'dp_1'}, dimensions={0}, use_global_device_ids=true | all-gather | bytes 49152 | tf_op jit(solution)/shard_map/all_gather | solution.py:31
  125.0 3.7 %all-gather.8 = f32[2,2,2048]{2,1,0:T(2,128)S(1)} all-gather(f32[1,2,2048]{2,1,0:T(2,128)S(1)} %maximum_bitcast_fusion.3), channel_id=5, replica_groups=mesh['section'=2,'dp_0'=8,'dp_1'=2,'vocab_0'=2,'vocab_1'=4] {'vocab_0'}, dimensions={0}, use_global_device_ids=true | all-gather | bytes 49152 | tf_op jit(solution)/shard_map/all_gather | solution.py:31
  128.7 10.5 %all-gather.9 = f32[4,2,2048]{2,1,0:T(2,128)S(1)} all-gather(f32[1,2,2048]{2,1,0:T(2,128)S(1)} %maximum_bitcast_fusion.4), channel_id=6, replica_groups=mesh['section'=2,'dp_0'=8,'dp_1'=2,'vocab_0'=2,'vocab_1'=4] {'vocab_1'}, dimensions={0}, use_global_device_ids=true | all-gather | bytes 81920 | tf_op jit(solution)/shard_map/all_gather | solution.py:31
  139.2 0.1 fusion.55
  139.3 2.5 %all-gather.15.cloned.1.call-done = bf16[2048,2048]{1,0:T(8,128)(2,1)} async-done(((bf16[128,2048]{1,0:T(8,128)(2,1)}), bf16[2048,2048]{1,0:T(8,128)(2,1)}) %all-gather.15.cloned.1.call-update) | async-done | bytes 8388624 | tf_op jit(solution)/shard_map/all_gather | solution.py:59
  141.7 6.0 %fusion.2 = f32[256,2048]{1,0:T(8,128)S(1)} fusion(bf16[2048,2048]{1,0:T(8,128)(2,1)} %all-gather.15.cloned.1.call-done, s32[2048]{0:T(1024)S(1)} %bitcast.279), kind=kOutput, calls=%fused_computation.7 | convolution fusion | flops 2148007936 | bytes 10493952 | tf_op jit(solution)/shard_map/dot_general | solution.py:97
  147.7 6.9 %fusion.1 = bf16[1,1,256,2048]{3,2,1,0:T(8,128)(2,1)} fusion(f32[256,2048]{1,0:T(8,128)S(1)} %fusion.2, bf16[2048,2048]{1,0:T(8,128)(2,1)} %all-gather.13.cloned.1.call-done, f32[2048,256]{0,1:T(8,128)S(1)} %copy-done.2, s32[2048]{0:T(1024)S(1)} %bitcast.278, f32[2048]{0:T(1024)S(1)} %get-tuple-element.5, f32[2048]{0:T(1024)S(1)} %get-tuple-element.6), kind=kOutput, calls=%fused_computation.2 | convolution fusion | flops 2151677952 | bytes 13656064 | tf_op jit(solution)/shard_map/dot_general | solution.py:94
  (15 shorter events, 0.3 us)
Async XLA Ops:
  6.5 77.7 %copy-start = (bf16[512,2048]{1,0:T(8,128)(2,1)S(1)}, bf16[512,2048]{1,0:T(8,128)(2,1)}, u32[]{:S(2)}) copy-start(bf16[512,2048]{1,0:T(8,128)(2,1)} %param.5) | copy-start | bytes 6291460
  6.5 17.5 %copy-start.3 = (s32[2,2048]{1,0:T(2,128)S(1)}, s32[2,2048]{1,0:T(2,128)}, u32[]{:S(2)}) copy-start(s32[2,2048]{1,0:T(2,128)} %param.4) | copy-start | bytes 49156
  6.5 77.7 %all-gather.13.cloned.1.call-start = ((), (), s32[]{:S(2)}) async-start(), calls=%async_computation | async-start | bytes 8912896 | tf_op jit(solution)/shard_map/all_gather | solution.py:60
  6.5 14.7 %collective-permute-start = (bf16[128,2048]{1,0:T(8,128)(2,1)}, bf16[128,2048]{1,0:T(8,128)(2,1)S(1)}, u32[]{:S(2)}, u32[]{:S(2)}) collective-permute-start(bf16[128,2048]{1,0:T(8,128)(2,1)} %bitcast.264), channel_id=1, source_target_pairs={{0,128},{128,0},{1,129},{129,1},{2,130},{130,2},{3,131},{131,3},{4... | collective-permute-start | bytes 1572872 | tf_op jit(solution)/shard_map/ppermute | solution.py:20
  23.3 118.4 %all-gather.15.cloned.1.call-start = ((), (), s32[]{:S(2)}) async-start(), calls=%async_computation.1 | async-start | bytes 8912896 | tf_op jit(solution)/shard_map/all_gather | solution.py:59
  90.0 1.3 copy-start.1
  141.7 6.0 %copy-start.2 = (f32[2048,256]{0,1:T(8,128)S(1)}, f32[2048,256]{0,1:T(8,128)}, u32[]{:S(2)}) copy-start(f32[2048,256]{0,1:T(8,128)} %copy-done.1) | copy-start | bytes 6291460
Sparse Core Ops, SparseCore 0:
  23.4 60.7 all-gather.12
  86.1 55.6 all-gather.14
where the time goes:
time: 162 us; the launch traced here: 161 us
  waiting for transfers between devices  74.2 us (46%)
  blocking collectives  47.1 us (29%)
  matrix products  18.6 us (11%)
  between operations  13.5 us (8%)
  starting transfers between devices  3.78 us (2%)
  other arithmetic  2.85 us (2%)
    all_gather x1, waiting for transfers between devices, spread_rows(): lax.all_gather(row_tuple[1], DP, axis=0, tiled=True)  60.1 us
    all_gather x5, blocking collectives, collected_together(): both, at, found = (lax.all_gather(jnp.concatenate(lines), axis), 0, {})  47.1 us
    ppermute x1, waiting for transfers between devices, from_partner(): return lax.ppermute(block, axis, route)  10.9 us
    dot_general x1, matrix products, body(): lax.dot_general(last_part, hid_all, (((0,), (0,)), ((), ())), preferred_e...  6.89 us
    dot_general x1, matrix products, body(): lax.dot_general(first_part, cot_all, (((0,), (0,)), ((), ())), preferred_...  5.97 us
    dot_general x1, matrix products, body(): lax.dot_general(hid_all, my_table, (((1,), (1,)), ((), ())), preferred_el...  5.75 us
    ppermute x1, starting transfers between devices, from_partner(): return lax.ppermute(block, axis, route)  3.73 us
  transfers between devices with their start and end apart: 3, of which 3 were waited for; matrix products, arithmetic and copies ran while one was open for 4% of the time, Pallas kernels for 0%

commit v1 on v0

--- a/solution.py
+++ b/solution.py
@@ -8,6 +8,11 @@
 VOCAB = ("vocab_0", "vocab_1")
 SECTION_DP_VOCAB = ("section", "dp_0", "dp_1", "vocab_0", "vocab_1")
 DP_VOCAB = ("dp_0", "dp_1", "vocab_0", "vocab_1")
+
+
+def gather_over(x, mesh_axis, d):
+    sent = jnp.stack([x] * lax.axis_size(mesh_axis))
+    return jnp.concatenate(lax.all_to_all(sent, mesh_axis, 0, 0), axis=d)
 
 
 def from_partner(block, axis, apart):
@@ -55,10 +60,7 @@
 
 
 def spread_rows(row_tuple):
-    return (
-        lax.all_gather(row_tuple[0], DP, axis=0, tiled=True),
-        lax.all_gather(row_tuple[1], DP, axis=0, tiled=True),
-    )
+    return (lax.all_gather(row_tuple[0], DP, axis=0, tiled=True), gather_over(row_tuple[1], DP, 0))
 
 
 def local_stats(logits):

time: 162 us -> 337 us (2.08)
  waiting for transfers between devices: 74.2 us -> 233 us
  starting transfers between devices: 3.78 us -> 14.6 us
  local copies, waits for them, and re-layouts: 1.39 us -> 5.68 us
    all_to_all x0 -> x1, waiting for transfers between devices: none -> 222 us  [gather_over(): return jnp.concatenate(lax.all_to_all(sent, mesh_axis, 0, 0), axis=d)]
    all_gather x1 -> x0, waiting for transfers between devices: 60.1 us -> none  [spread_rows(): lax.all_gather(row_tuple[1], DP, axis=0, tiled=True)]
    all_to_all x0 -> x1, starting transfers between devices: none -> 10.8 us  [gather_over(): return jnp.concatenate(lax.all_to_all(sent, mesh_axis, 0, 0), axis=d)]
    another operation x0 -> x1, local copies, waits for them, and re-layouts: none -> 4.29 us  [gather_over(): sent = jnp.stack([x] * lax.axis_size(mesh_axis))]
  transfers between devices with their start and end apart: 3 -> 3, of which waited for: 3 -> 2; matrix products, arithmetic and copies ran while one was open for 4% -> 2% of each run, Pallas kernels for 0% -> 0%
where the time goes in v1:
time: 337 us; the launch traced here: 334 us
  waiting for transfers between devices  233 us (69%)
  blocking collectives  45.5 us (14%)
  matrix products  18.6 us (6%)
  starting transfers between devices  14.6 us (4%)
  between operations  13.5 us (4%)
  local copies, waits for them, and re-layouts  5.68 us (2%)
    all_to_all x1, waiting for transfers between devices, gather_over(): return jnp.concatenate(lax.all_to_all(sent, mesh_axis, 0, 0), axis=d)  222 us
    all_gather x5, blocking collectives, collected_together(): both, at, found = (lax.all_gather(jnp.concatenate(lines), axis), 0, {})  45.5 us
    ppermute x1, waiting for transfers between devices, from_partner(): return lax.ppermute(block, axis, route)  10.9 us
    all_to_all x1, starting transfers between devices, gather_over(): return jnp.concatenate(lax.all_to_all(sent, mesh_axis, 0, 0), axis=d)  10.8 us
    dot_general x1, matrix products, body(): lax.dot_general(last_part, hid_all, (((0,), (0,)), ((), ())), preferred_e...  6.89 us
  transfers between devices with their start and end apart: 3, of which 2 were waited for; matrix products, arithmetic and copies ran while one was open for 2% of the time, Pallas kernels for 0%

profile of v1, /device:TPU:1, one launch (start us, length us, event | category | flops | bytes accessed | tf_op | source)
XLA Modules:
  0.0 334.1 jit_solution(14460027204776036557)
XLA Ops:
  6.5 0.0 copy-start
  6.5 3.7 %collective-permute-start = (bf16[128,2048]{1,0:T(8,128)(2,1)}, bf16[128,2048]{1,0:T(8,128)(2,1)S(1)}, u32[]{:S(2)}, u32[]{:S(2)}) collective-permute-start(bf16[128,2048]{1,0:T(8,128)(2,1)} %bitcast.265), channel_id=1, source_target_pairs={{0,128},{128,0},{1,129},{129,1},{2,130},{130,2},{3,131},{131,3},{4... | collective-permute-start | bytes 1572872 | tf_op jit(solution)/shard_map/ppermute | solution.py:25
  10.3 10.9 %collective-permute-done = bf16[128,2048]{1,0:T(8,128)(2,1)S(1)} collective-permute-done((bf16[128,2048]{1,0:T(8,128)(2,1)}, bf16[128,2048]{1,0:T(8,128)(2,1)S(1)}, u32[]{:S(2)}, u32[]{:S(2)}) %collective-permute-start) | collective-permute-done | bytes 524320 | tf_op jit(solution)/shard_map/ppermute | solution.py:25
  21.2 1.9 broadcast_select_fusion.1
  23.1 4.3 %stack.2 = bf16[16,128,2048]{2,1,0:T(8,128)(2,1)} broadcast(bf16[128,2048]{1,0:T(8,128)(2,1)S(1)} %get-tuple-element.17), dimensions={1,2} | broadcast | bytes 8912896 | tf_op jit(solution)/shard_map/stack | solution.py:14
  27.4 10.8 %all-to-all-start = ((bf16[16,128,2048]{2,1,0:T(8,128)(2,1)}), bf16[16,128,2048]{2,1,0:T(8,128)(2,1)}, u32[]{:S(2)}, u32[]{:S(2)}) async-start(bf16[16,128,2048]{2,1,0:T(8,128)(2,1)} %stack.2), calls=%async_computation | async-start | bytes 16777216 | tf_op jit(solution)/shard_map/all_to_all | solution.py:15
  38.2 0.0 all-gather.12.cloned.1.call-start
  38.3 0.7 all-gather.12.cloned.1.call-update
  39.0 0.0 copy-done.3
  39.0 221.9 %all-to-all-done = bf16[16,128,2048]{2,1,0:T(8,128)(2,1)} async-done(((bf16[16,128,2048]{2,1,0:T(8,128)(2,1)}), bf16[16,128,2048]{2,1,0:T(8,128)(2,1)}, u32[]{:S(2)}, u32[]{:S(2)}) %all-to-all-start) | async-done | bytes 8388640 | tf_op jit(solution)/shard_map/all_to_all | solution.py:15
  260.9 5.8 %fusion.56 = (f32[2048]{0:T(1024)S(1)}, f32[2048,256]{0,1:T(8,128)S(1)}) fusion(bf16[2048,2048]{1,0:T(8,128)(2,1)} %bitcast.1, bf16[512,2048]{1,0:T(8,128)(2,1)S(1)} %copy-done, s32[]{:T(128)S(6)} %select_n.17), kind=kOutput, calls=%fused_computation.95 | convolution fusion | flops 2148005888 | bytes 11542532 | tf_op jit(solution)/shard_map/dot_general | solution.py:88
  266.6 1.3 copy-done.1
  268.0 0.3 exponential_reduce_fusion
  268.3 4.8 %all-gather.5 = f32[2,2,2048]{2,1,0:T(2,128)S(1)} all-gather(f32[1,2,2048]{2,1,0:T(2,128)S(1)} %maximum_bitcast_fusion), channel_id=2, replica_groups=mesh['section'=2,'dp_0'=8,'dp_1'=2,'vocab_0'=2,'vocab_1'=4] {'section'}, dimensions={0}, use_global_device_ids=true | all-gather | bytes 49152 | tf_op jit(solution)/shard_map/all_gather | solution.py:36
  273.1 18.3 %all-gather.6 = f32[8,2,2048]{2,1,0:T(2,128)S(1)} all-gather(f32[1,2,2048]{2,1,0:T(2,128)S(1)} %maximum_bitcast_fusion.1), channel_id=3, replica_groups=mesh['section'=2,'dp_0'=8,'dp_1'=2,'vocab_0'=2,'vocab_1'=4] {'dp_0'}, dimensions={0}, use_global_device_ids=true | all-gather | bytes 147456 | tf_op jit(solution)/shard_map/all_gather | solution.py:36
  291.4 0.2 fusion.16
  291.6 9.9 %all-gather.7 = f32[2,2,2048]{2,1,0:T(2,128)S(1)} all-gather(f32[1,2,2048]{2,1,0:T(2,128)S(1)} %maximum_bitcast_fusion.2), channel_id=4, replica_groups=mesh['section'=2,'dp_0'=8,'dp_1'=2,'vocab_0'=2,'vocab_1'=4] {'dp_1'}, dimensions={0}, use_global_device_ids=true | all-gather | bytes 49152 | tf_op jit(solution)/shard_map/all_gather | solution.py:36
  301.6 3.3 all-gather.8
  304.9 9.3 %all-gather.9 = f32[4,2,2048]{2,1,0:T(2,128)S(1)} all-gather(f32[1,2,2048]{2,1,0:T(2,128)S(1)} %maximum_bitcast_fusion.4), channel_id=6, replica_groups=mesh['section'=2,'dp_0'=8,'dp_1'=2,'vocab_0'=2,'vocab_1'=4] {'vocab_1'}, dimensions={0}, use_global_device_ids=true | all-gather | bytes 81920 | tf_op jit(solution)/shard_map/all_gather | solution.py:36
  314.2 0.1 fusion.55
  314.3 0.0 all-gather.12.cloned.1.call-done
  314.4 0.0 copy-start.2
  314.4 6.0 %fusion.2 = f32[256,2048]{1,0:T(8,128)S(1)} fusion(bf16[2048,2048]{1,0:T(8,128)(2,1)} %all-gather.12.cloned.1.call-done, s32[2048]{0:T(1024)S(1)} %bitcast.280), kind=kOutput, calls=%fused_computation.7 | convolution fusion | flops 2148007936 | bytes 10493952 | tf_op jit(solution)/shard_map/dot_general | solution.py:99
  320.3 6.9 %fusion.1 = bf16[1,1,256,2048]{3,2,1,0:T(8,128)(2,1)} fusion(f32[256,2048]{1,0:T(8,128)S(1)} %fusion.2, bf16[2048,2048]{1,0:T(8,128)(2,1)} %bitcast.1, f32[2048,256]{0,1:T(8,128)S(1)} %copy-done.2, s32[2048]{0:T(1024)S(1)} %bitcast.279, f32[2048]{0:T(1024)S(1)} %get-tuple-element.5, f32[2048]{0:T(1024)S(1)} %get-tuple-element.6), kind=kOutput, calls=%fused_computation.2 | convolution fusion | flops 2151677952 | bytes 13656064 | tf_op jit(solution)/shard_map/dot_general | solution.py:96
  (15 shorter events, 0.3 us)
Async XLA Ops:
  6.5 254.3 %copy-start = (bf16[512,2048]{1,0:T(8,128)(2,1)S(1)}, bf16[512,2048]{1,0:T(8,128)(2,1)}, u32[]{:S(2)}) copy-start(bf16[512,2048]{1,0:T(8,128)(2,1)} %param.5) | copy-start | bytes 6291460
  6.5 14.7 %collective-permute-start = (bf16[128,2048]{1,0:T(8,128)(2,1)}, bf16[128,2048]{1,0:T(8,128)(2,1)S(1)}, u32[]{:S(2)}, u32[]{:S(2)}) collective-permute-start(bf16[128,2048]{1,0:T(8,128)(2,1)} %bitcast.265), channel_id=1, source_target_pairs={{0,128},{128,0},{1,129},{129,1},{2,130},{130,2},{3,131},{131,3},{4... | collective-permute-start | bytes 1572872 | tf_op jit(solution)/shard_map/ppermute | solution.py:25
  27.4 11.6 %copy-start.3 = (s32[2,2048]{1,0:T(2,128)S(1)}, s32[2,2048]{1,0:T(2,128)}, u32[]{:S(2)}) copy-start(s32[2,2048]{1,0:T(2,128)} %param.4) | copy-start | bytes 49156
  27.4 233.5 %all-to-all-start = ((bf16[16,128,2048]{2,1,0:T(8,128)(2,1)}), bf16[16,128,2048]{2,1,0:T(8,128)(2,1)}, u32[]{:S(2)}, u32[]{:S(2)}) async-start(bf16[16,128,2048]{2,1,0:T(8,128)(2,1)} %stack.2), calls=%async_computation | async-start | bytes 16777216 | tf_op jit(solution)/shard_map/all_to_all | solution.py:15
  38.2 276.1 %all-gather.12.cloned.1.call-start = ((), (), s32[]{:S(2)}) async-start(), calls=%async_computation.1 | async-start | bytes 8912896 | tf_op jit(solution)/shard_map/all_gather | solution.py:63
  266.6 1.3 copy-start.1
  314.4 6.0 %copy-start.2 = (f32[2048,256]{0,1:T(8,128)S(1)}, f32[2048,256]{0,1:T(8,128)}, u32[]{:S(2)}) copy-start(f32[2048,256]{0,1:T(8,128)} %copy-done.1) | copy-start | bytes 6291460
Sparse Core Ops, SparseCore 0:
  40.9 167.6 all-gather.11
